TPU v7x, 32 devices: a whole 2x2x4 slice. The times are simulated.
32 devices in a mesh: dp: 8 (over z, y), tp: 4 (over x, core).
Axes of the slice: x: 2, y: 2, z: 4, core: 2. Of those that a mesh axis runs over, the one named last changes fastest.
Arguments:
- queries: bfloat16 [2048, 4096], P('dp', 'tp'), may hold values from -6 to 6
- keys: bfloat16 [2048, 512], P(('dp', 'tp')), may hold values from -6 to 6
- values: bfloat16 [2048, 512], P(('dp', 'tp')), may hold values from -6 to 6
- out_weight: bfloat16 [4096, 8192], P('tp', 'dp'), may hold values from -0.09375 to 0.09375
- residual: bfloat16 [2048, 8192], P(('dp', 'tp')), may hold values from -40 to 40
- norm_gain: float32 [8192], replicated, may hold values from 0.5 to 1.5
Outputs:
- hidden_out: bfloat16 [2048, 8192], P(('dp', 'tp'))
- normed: bfloat16 [2048, 8192], P(('dp', 'tp'))
All inputs are finite; a program needn't handle non-finite values.
Results may differ from a plain program's by a relative error of at most 0.012.
Values may be sent and summed in bfloat16 or wider, within the bound.
A program may use at most 64 MiB of HBM per device.

v0:
```python
import math

import jax
import jax.numpy as jnp
from jax import lax
from jax.sharding import PartitionSpec as P

KVH = 4
HDIM = 128
LEN = 32


def attention(queries, key_head, value_head):
    rows = queries.shape[0]
    sequences = rows // LEN
    local_heads = queries.shape[1] // HDIM
    query_heads = queries.reshape(sequences, LEN, local_heads, HDIM)
    key_rows = key_head.reshape(sequences, LEN, HDIM)
    value_rows = value_head.reshape(sequences, LEN, HDIM)
    scores = jnp.einsum(
        "slhd,smd->shlm", query_heads, key_rows, preferred_element_type=jnp.float32
    ) / math.sqrt(HDIM)
    causal = jnp.arange(LEN)[:, None] >= jnp.arange(LEN)[None, :]
    scores = jnp.where(causal, scores, -1e30)
    highest = jnp.max(scores, axis=-1, keepdims=True)
    powers = jnp.exp(scores - highest)
    weights = (powers / jnp.sum(powers, axis=-1, keepdims=True)).astype(jnp.bfloat16)
    attended = jnp.einsum("shlm,smd->slhd", weights, value_rows, preferred_element_type=jnp.float32)
    return attended.astype(jnp.bfloat16).reshape(rows, local_heads * HDIM)


def local(queries, keys, values, out_weight, residual, norm_gain):
    tp_size = lax.axis_size("tp")
    position = lax.axis_index("tp")
    gathered_keys, gathered_values = (
        lax.all_gather(keys, "tp", axis=0, tiled=True),
        lax.all_gather(values, "tp", axis=0, tiled=True),
    )
    head = position * KVH // tp_size
    key_head = lax.dynamic_slice_in_dim(gathered_keys, head * HDIM, HDIM, 1)
    value_head = lax.dynamic_slice_in_dim(gathered_values, head * HDIM, HDIM, 1)
    attended = attention(queries, key_head, value_head)
    partial_value = jnp.dot(
        attended,
        lax.all_gather(out_weight, "dp", axis=1, tiled=True),
        preferred_element_type=jnp.float32,
    )
    projected = lax.psum_scatter(
        partial_value.astype(jnp.bfloat16), "tp", scatter_dimension=0, tiled=True
    ).astype(jnp.float32)
    updated = residual.astype(jnp.float32) + projected
    hidden_out = updated.astype(jnp.bfloat16)
    meansq = jnp.mean(updated * updated, axis=-1, keepdims=True)
    normed = (updated * lax.rsqrt(meansq + 1e-05) * norm_gain).astype(jnp.bfloat16)
    return (hidden_out, normed)


def solution(mesh):
    return jax.shard_map(
        local,
        mesh=mesh,
        in_specs=(
            P("dp", "tp"),
            P(("dp", "tp"), None),
            P(("dp", "tp"), None),
            P("tp", "dp"),
            P(("dp", "tp"), None),
            P(),
        ),
        out_specs=(P(("dp", "tp"), None), P(("dp", "tp"), None)),
        check_vma=False,
    )
```

profile of v0, /device:TPU:0, one launch (start us, length us, event | category | flops | bytes accessed | tf_op | source)
XLA Modules:
  0.0 305.3 jit_solution(16371543206600074251)
XLA Ops:
  7.2 0.0 copy-start.2
  7.2 0.0 copy-start.3
  7.2 0.0 copy-start.4
  7.2 0.0 all-gather.2.cloned.1.call-start
  7.2 0.7 all-gather.2.cloned.1.call-update
  7.9 0.0 reduce-scatter.2.cloned.1.call-start
  8.0 0.2 copy-done.2
  8.2 0.1 copy.16
  8.3 0.0 copy-done.3
  8.3 7.2 %all_gather.10 = bf16[256,512]{1,0:T(8,128)(2,1)S(1)} all-gather(bf16[64,512]{1,0:T(8,128)(2,1)S(1)} %copy-done.3), channel_id=1, replica_groups=mesh['dp'=8,'tp'=4] {'tp'}, dimensions={0}, use_global_device_ids=true | all-gather | bytes 327680 | tf_op jit(solution)/shard_map/all_gather | solution.py:36
  15.5 0.0 copy-done.4
  15.5 5.8 %all_gather.9 = bf16[256,512]{1,0:T(8,128)(2,1)S(1)} all-gather(bf16[64,512]{1,0:T(8,128)(2,1)S(1)} %copy-done.4), channel_id=1, replica_groups=mesh['dp'=8,'tp'=4] {'tp'}, dimensions={0}, use_global_device_ids=true | all-gather | bytes 327680 | tf_op jit(solution)/shard_map/all_gather | solution.py:37
  21.4 1.0 fusion.15
  22.4 0.9 fusion.5
  23.3 0.5 fusion.6
  23.8 0.2 copy.12
  24.0 216.2 %all-gather.2.cloned.1.call-done = bf16[1024,8192]{1,0:T(8,128)(2,1)} async-done(((bf16[1024,1024]{1,0:T(8,128)(2,1)}), bf16[1024,8192]{1,0:T(8,128)(2,1)}) %all-gather.2.cloned.1.call-update) | async-done | bytes 16777232 | tf_op jit(solution)/shard_map/all_gather | solution.py:45
  240.2 11.8 %convolution_convert_fusion = bf16[256,8192]{1,0:T(8,128)(2,1)} fusion(bf16[1024,8192]{1,0:T(8,128)(2,1)} %all-gather.2.cloned.1.call-done, bf16[32,8,8,128]{3,2,1,0:T(8,128)(2,1)S(1)} %bitcast.36), kind=kOutput, calls=%fused_computation.1 | convolution fusion | flops 4297064448 | bytes 21495808 | tf_op jit(solution)/shard_map/dot_general | solution.py:43
  252.0 0.0 reduce-scatter.2.cloned.1.call-update
  252.0 0.0 copy-start.5
  252.0 42.9 %reduce-scatter.2.cloned.1.call-done = bf16[64,8192]{1,0:T(8,128)(2,1)} async-done(((bf16[256,8192]{1,0:T(8,128)(2,1)}), bf16[64,8192]{1,0:T(8,128)(2,1)}) %reduce-scatter.2.cloned.1.call-update) | async-done | bytes 1048592 | tf_op jit(solution)/shard_map/reduce_scatter | solution.py:48
  294.9 0.0 copy-done
  294.9 1.8 multiply_reduce_fusion
  296.7 1.8 multiply_convert_fusion
  (8 shorter events, 0.0 us)
Async XLA Ops:
  7.2 1.0 copy-start.2
  7.2 1.1 copy-start.3
  7.2 8.4 %copy-start.4 = (bf16[64,512]{1,0:T(8,128)(2,1)S(1)}, bf16[64,512]{1,0:T(8,128)(2,1)}, u32[]{:S(2)}) copy-start(bf16[64,512]{1,0:T(8,128)(2,1)} %param.8) | copy-start | bytes 196612
  7.2 233.0 %all-gather.2.cloned.1.call-start = ((), (), s32[]{:S(2)}) async-start(), calls=%async_computation.1 | async-start | bytes 18874368 | tf_op jit(solution)/shard_map/all_gather | solution.py:45
  7.9 287.0 %reduce-scatter.2.cloned.1.call-start = ((), (), s32[]{:S(2)}) async-start(), calls=%async_computation.2 | async-start | bytes 5242880 | tf_op jit(solution)/shard_map/reduce_scatter | solution.py:48
  252.0 42.9 %copy-start = (bf16[64,8192]{1,0:T(8,128)(2,1)S(1)}, bf16[64,8192]{1,0:T(8,128)(2,1)}, u32[]{:S(2)}) copy-start(bf16[64,8192]{1,0:T(8,128)(2,1)} %param.10) | copy-start | bytes 3145732
  252.0 44.7 %copy-start.5 = (f32[8192]{0:T(1024)S(1)}, f32[8192]{0:T(1024)}, u32[]{:S(2)}) copy-start(f32[8192]{0:T(1024)} %param.11) | copy-start | bytes 98308
  294.9 1.8 copy-start.1
Sparse Core Ops, SparseCore 0:
  10.2 229.9 all-gather.1
  252.1 42.7 reduce-scatter.1
where the time goes:
time: 306 us; the launch traced here: 305 us
  waiting for transfers between devices  260 us (85%)
  between operations  14.2 us (5%)
  matrix products  14.1 us (5%)
  blocking collectives  13.1 us (4%)
  other arithmetic  3.53 us (1%)
    all_gather x1, waiting for transfers between devices, local(): lax.all_gather(out_weight, 'dp', axis=1, tiled=True)  216 us
    reduce_scatter x1, waiting for transfers between devices, local(): lax.psum_scatter(partial_value.astype(jnp.bfloat16), 'tp', scatter_dimens...  42.9 us
    dot_general x1, matrix products, local(): jnp.dot(attended, lax.all_gather(out_weight, 'dp', axis=1, tiled=True), p...  11.8 us
    all_gather x1, blocking collectives, local(): lax.all_gather(keys, 'tp', axis=0, tiled=True)  7.22 us
  transfers between devices with their start and end apart: 2, of which 2 were waited for; matrix products, arithmetic and copies ran while one was open for 1% of the time, Pallas kernels for 0%

commit v1 on v0

v1 whole, which is shorter than its diff:
```python
import functools
import math

import jax
import jax.numpy as jnp
from jax import lax
from jax.experimental import pallas as pl
from jax.experimental.pallas import tpu as pltpu
from jax.sharding import PartitionSpec as P

KVH = 4
HDIM = 128
LEN = 32
MESH = pl.DeviceIdType.MESH
BF = jnp.bfloat16
F32 = jnp.float32


def flip(value, mask, bits):
    for bit in range(bits):
        step = 1 << bit
        if mask & step:
            value = value + step - 2 * step * ((value // step) % 2)
    return value


def reverse(value, bits):
    return sum(((value >> bit) & 1) << (bits - 1 - bit) for bit in range(bits))


def pick(index, table):
    result = jnp.int32(table[0])
    for at, entry in enumerate(table[1:], 1):
        result = jnp.where(index == at, jnp.int32(entry), result)
    return result


def visit_order(at, line):
    return sorted(range(line), key=lambda other: (abs(other - at), (other > at) == (at * 2 < line - 1)))


def plan(line, blocks, pieces, halves, stages):
    hop, start, weights = 11.0, 8.0, 42.0
    events = []
    for k in range(1, line):
        for half in range(halves):
            distance = (k + 1) // 2
            events.append((start + hop * (distance - 1) + hop * (half + 1) / halves, 0, ("forward", k, half)))
    units = []
    for k in range(line):
        for c in range(blocks * pieces):
            there = 0.0 if c < pieces else 3.0 + weights * (c - pieces + 1) / (blocks * pieces - pieces)
            units.append((max(start + hop * k, there), k, c))
    units.sort()
    clock = 0.0
    for number, (when, k, c) in enumerate(units):
        clock = max(when, clock + 0.7)
        events.append((clock, 1, ("unit", number, 0)))
        for stage in range(1, stages + 1):
            events.append((clock + (1.5 if stage == 1 else 1.5 + 2.5 * (stage - 1)), 2 + stage, ("stage", number, stage)))
    events.sort()
    return [(k, c) for _, k, c in units], [event for _, _, event in events]


def kernel(cfg, q_ref, k_ref, v_ref, w_ref, r_ref, g_ref, hid_ref, nrm_ref,
           q_v, k_v, v_v, att, w_v, r_v, g_v, keeps, sends, recvs, fin, fin_snd, upd, hid_v, nrm_v,
           loc_sem, kv_snd, kv_rcv, g_snd, g_rcv, w_snd, w_rcv, s_snd, s_rcv, f_snd, f_rcv, o_sem):
    tp, dp, line, blocks, pieces, halves, stages = cfg
    rows, width = q_v.shape
    cols = w_v.shape[2]
    own_cols = cols * pieces
    tok = rows // tp
    features = fin.shape[1]
    me_dp, me = lax.axis_index("dp"), lax.axis_index("tp")
    a, b = me_dp // blocks, me_dp % blocks
    slot = [reverse(i, stages) for i in range(tp)]

    def dev(aa, bb, tt):
        return (aa * blocks + bb, tt)

    def remote(src, dst, snd, rcv, device):
        return pltpu.make_async_remote_copy(
            src_ref=src, dst_ref=dst, send_sem=snd, recv_sem=rcv, device_id=device, device_id_type=MESH)

    def aligned(value, unit):
        return pl.ds(pl.multiple_of(value, unit), unit)

    locals_ = []

    def local(src, dst):
        copy = pltpu.make_async_copy(src, dst, loc_sem.at[len(locals_)])
        copy.start()
        locals_.append(copy)
        return copy

    head = me * KVH // tp
    first = []
    for i in range(tp):
        first.append(local(q_ref.at[aligned(flip(me, i, stages) * tok, tok)], q_v.at[pl.ds(slot[i] * tok, tok)]))
    first.append(local(k_ref.at[:, aligned(head * HDIM, HDIM)], k_v.at[pl.ds(0, tok)]))
    first.append(local(v_ref.at[:, aligned(head * HDIM, HDIM)], v_v.at[pl.ds(0, tok)]))
    w_local = [local(w_ref.at[:, pl.ds(s * cols, cols)], w_v.at[s]) for s in range(pieces)]
    r_local = [local(r_ref, r_v), local(g_ref, g_v)]

    barrier = pltpu.get_barrier_semaphore()
    order = [pick(a, [visit_order(at, line)[k] for at in range(line)]) for k in range(line)]
    for i in range(1, tp):
        pl.semaphore_signal(barrier, inc=1, device_id=dev(a, b, flip(me, i, stages)), device_id_type=MESH)
    for j in range(1, blocks):
        pl.semaphore_signal(barrier, inc=1, device_id=dev(a, (b + j) % blocks, me), device_id_type=MESH)
    for k in range(1, line):
        pl.semaphore_signal(barrier, inc=1, device_id=dev(order[k], b, me), device_id_type=MESH)
    pl.semaphore_wait(barrier, tp - 1 + blocks - 1 + line - 1)

    kv = []
    for i in range(1, tp):
        peer = flip(me, i, stages)
        lanes = aligned((peer * KVH // tp) * HDIM, HDIM)
        for n, (src, dst) in enumerate(((k_ref, k_v), (v_ref, v_v))):
            copy = remote(src.at[:, lanes], dst.at[pl.ds(slot[i] * tok, tok)],
                          kv_snd.at[n, i], kv_rcv.at[n, i], dev(a, b, peer))
            copy.start()
            kv.append(copy)

    w_copies = {}
    for j in range(1, blocks):
        for s in range(pieces):
            c = j * pieces + s
            copy = remote(w_ref.at[:, pl.ds(s * cols, cols)], w_v.at[c], w_snd.at[c], w_rcv.at[c],
                          dev(a, (b + blocks - j) % blocks, me))
            copy.start()
            w_copies[c] = copy

    for copy in first:
        copy.wait()
    for copy in kv:
        copy.wait_recv()

    size = rows // halves
    heads = width // HDIM

    def token(index):
        block = index // tok
        where = jnp.zeros_like(index)
        for bit in range(stages):
            mine = (me // (1 << bit)) % 2
            theirs = (block // (1 << (stages - 1 - bit))) % 2
            where = where + (1 << bit) * ((mine + theirs) % 2)
        return where * tok + index % tok

    def att_part(source, half):
        return att.at[source, pl.ds(half * size, size)]

    def hop(source, half, target, way):
        part = att_part(source, half)
        return remote(part, part, g_snd.at[source, half, way], g_rcv.at[source, half], dev(target, b, me))

    def line_send(source, half, down, up):
        @pl.when(down)
        def _():
            hop(source, half, a - 1, 0).start()

        @pl.when(up)
        def _():
            hop(source, half, a + 1, 1).start()

    for half in range(halves):
        part = pl.ds(half * size, size)
        row = lax.broadcasted_iota(jnp.int32, (size, size), 0)
        col = lax.broadcasted_iota(jnp.int32, (size, size), 1)
        if tok % LEN:
            row, col = token(row + half * size), token(col + half * size)
        seen = (row // LEN == col // LEN) & (row >= col)
        keys, vals = k_v[part, :], v_v[part, :]
        for h in range(heads):
            lanes = pl.ds(h * HDIM, HDIM)
            scores = lax.dot_general(q_v[part, lanes], keys, (((1,), (1,)), ((), ())),
                                     preferred_element_type=F32) / math.sqrt(HDIM)
            scores = jnp.where(seen, scores, -1e30)
            powers = jnp.exp(scores - jnp.max(scores, axis=-1, keepdims=True))
            probs = (powers / jnp.sum(powers, axis=-1, keepdims=True)).astype(BF)
            att[a, part, lanes] = jnp.dot(probs, vals, preferred_element_type=F32).astype(BF)
        line_send(a, half, a > 0, a < line - 1)

    for copy in w_local:
        copy.wait()

    units, events = plan(line, blocks, pieces, halves, stages)
    have_w, have_k = set(range(pieces)), {0}

    def passes(k):
        source = order[k]
        down = jnp.logical_and(source > a, a > 0)
        up = jnp.logical_and(source < a, a < line - 1)
        return source, down, up

    def finish(number, total):
        k, c = units[number]
        j, s = divmod(c, pieces)
        start = (a * blocks + (b + j) % blocks) * own_cols + s * cols
        lanes = aligned(start, cols)
        if k == 0:
            fin[:, lanes] = total.astype(BF)
            return
        fin_snd[number] = total.astype(BF)
        remote(fin_snd.at[number], fin.at[:, lanes], f_snd.at[number], f_rcv.at[a, c], dev(order[k], b, me)).start()

    def exchange(number, stage):
        return remote(sends[stage].at[number], recvs[stage].at[number], s_snd.at[stage, number],
                      s_rcv.at[stage, number], dev(a, b, flip(me, 1 << stage, stages)))

    def pass_on(number, stage, total):
        if stage == stages:
            finish(number, total)
            return
        mid = total.shape[0] // 2
        sends[stage][number] = total[mid:].astype(BF)
        exchange(number, stage).start()
        keeps[stage][number] = total[:mid]

    for kind, number, extra in events:
        if kind == "forward":
            source, down, up = passes(number)

            @pl.when(jnp.logical_or(down, up))
            def _():
                hop(source, extra, a, 0).wait_recv()

            line_send(source, extra, down, up)
        elif kind == "unit":
            k, c = units[number]
            source, down, up = passes(k)
            if k not in have_k:
                have_k.add(k)

                @pl.when(jnp.logical_not(jnp.logical_or(down, up)))
                def _():
                    for half in range(halves):
                        hop(source, half, a, 0).wait_recv()

            if c not in have_w:
                have_w.add(c)
                w_copies[c].wait_recv()
            pass_on(number, 0, jnp.dot(att[source], w_v[c], preferred_element_type=F32))
        else:
            exchange(number, extra - 1).wait_recv()
            total = keeps[extra - 1][number] + recvs[extra - 1][number].astype(F32)
            pass_on(number, extra, total)

    for copy in r_local:
        copy.wait()
    squares = jnp.zeros((tok, 1), F32)

    for k in range(line):
        source = order[k]
        for c in range(blocks * pieces):
            j, s = divmod(c, pieces)
            lanes = aligned((source * blocks + (b + j) % blocks) * own_cols + s * cols, cols)
            if k:
                remote(fin.at[:, lanes], fin.at[:, lanes], f_snd.at[0], f_rcv.at[source, c],
                       dev(source, b, me)).wait_recv()
            now = r_v[:, lanes].astype(F32) + fin[:, lanes].astype(F32)
            upd[:, lanes] = now
            hid_v[:, lanes] = now.astype(BF)
            squares = squares + jnp.sum(now * now, axis=-1, keepdims=True)
    out_h = pltpu.make_async_copy(hid_v, hid_ref, o_sem.at[0])
    out_h.start()
    scale = lax.rsqrt(squares / features + 1e-05)
    step = min(features, 1024)
    for n in range(features // step):
        lanes = pl.ds(n * step, step)
        nrm_v[:, lanes] = (upd[:, lanes] * scale * g_v[:, lanes]).astype(BF)
    out_n = pltpu.make_async_copy(nrm_v, nrm_ref, o_sem.at[1])
    out_n.start()

    for copy in kv:
        copy.wait_send()
    for copy in w_copies.values():
        copy.wait_send()
    for k in range(line):
        if k:
            source, down, up = passes(k)
        else:
            source, down, up = a, a > 0, a < line - 1
        for half in range(halves):
            @pl.when(down)
            def _():
                hop(source, half, a - 1, 0).wait_send()

            @pl.when(up)
            def _():
                hop(source, half, a + 1, 1).wait_send()
    for number, (k, c) in enumerate(units):
        for stage in range(stages):
            exchange(number, stage).wait_send()
        if k:
            remote(fin_snd.at[number], fin.at[:, pl.ds(0, cols)], f_snd.at[number], f_rcv.at[a, c],
                   dev(order[k], b, me)).wait_send()
    out_h.wait()
    out_n.wait()


def local(tp, dp, queries, keys, values, out_weight, residual, norm_gain):
    rows, width = queries.shape
    own_cols = out_weight.shape[1]
    tok, features = residual.shape
    blocks = 2 if dp % 2 == 0 else 1
    line = dp // blocks
    pieces = max(1, min(2, own_cols // 256))
    cols = own_cols // pieces
    halves = 2 if tok % LEN == 0 else 1
    stages = tp.bit_length() - 1
    chunks = blocks * pieces
    count = line * chunks
    any_ = pl.BlockSpec(memory_space=pl.ANY)
    vm = pltpu.VMEM
    dma = pltpu.SemaphoreType.DMA
    cfg = (tp, dp, line, blocks, pieces, halves, stages)
    parts = [rows >> (stage + 1) for stage in range(stages)]
    out = jax.ShapeDtypeStruct((tok, features), BF)
    return pl.pallas_call(
        functools.partial(kernel, cfg),
        out_shape=(out, out),
        in_specs=[any_] * 6,
        out_specs=(any_, any_),
        scratch_shapes=[
            vm((rows, width), BF), vm((rows, HDIM), BF), vm((rows, HDIM), BF),
            vm((line, rows, width), BF), vm((chunks, width, cols), BF),
            vm((tok, features), BF), vm((1, features), F32),
            tuple(vm((count, part, cols), F32) for part in parts),
            tuple(vm((count, part, cols), BF) for part in parts),
            tuple(vm((count, part, cols), BF) for part in parts),
            vm((tok, features), BF), vm((count, tok, cols), BF), vm((tok, features), F32),
            vm((tok, features), BF), vm((tok, features), BF),
            dma((tp + 4 + pieces,)), dma((2, tp)), dma((2, tp)),
            dma((line, halves, 2)), dma((line, halves)), dma((chunks,)), dma((chunks,)),
            dma((stages, count)), dma((stages, count)), dma((count,)), dma((line, chunks)), dma((2,)),
        ],
        compiler_params=pltpu.CompilerParams(
            collective_id=0, has_side_effects=True, vmem_limit_bytes=56 * 1024 * 1024),
    )(queries, keys, values, out_weight, residual, norm_gain.reshape(1, features))


def solution(mesh):
    return jax.shard_map(
        functools.partial(local, mesh.shape["tp"], mesh.shape["dp"]),
        mesh=mesh,
        in_specs=(
            P("dp", "tp"),
            P(("dp", "tp"), None),
            P(("dp", "tp"), None),
            P("tp", "dp"),
            P(("dp", "tp"), None),
            P(),
        ),
        out_specs=(P(("dp", "tp"), None), P(("dp", "tp"), None)),
        check_vma=False,
    )
```

time: 306 us -> 77.2 us (0.25)
  waiting for transfers between devices: 260 us -> 0 us
  Pallas kernels: 0 us -> 73.1 us
  matrix products: 14.1 us -> 0 us
  between operations: 14.2 us -> 0.65 us
  blocking collectives: 13.1 us -> 0 us
  other arithmetic: 3.53 us -> 0 us
    all_gather x1 -> x0, waiting for transfers between devices: 216 us -> none  [local(): lax.all_gather(out_weight, 'dp', axis=1, tiled=True)]
    pallas_call x0 -> x1, Pallas kernels: none -> 73.1 us  [local(): pl.pallas_call(functools.partial(kernel, cfg), out_shape=(out, out), in_s...]
    reduce_scatter x1 -> x0, waiting for transfers between devices: 42.9 us -> none  [local(): lax.psum_scatter(partial_value.astype(jnp.bfloat16), 'tp', scatter_dimens...]
    dot_general x3 -> x0, matrix products: 13.2 us -> none  [the longest x1 11.8 us: local(): jnp.dot(attended, lax.all_gather(out_weight, 'dp', axis=1, tiled=True), p...]
    all_gather x2 -> x0, blocking collectives: 13.1 us -> none  [the longest x1 7.22 us: local(): lax.all_gather(keys, 'tp', axis=0, tiled=True)]
  transfers between devices with their start and end apart: 2 -> 0, of which waited for: 2 -> 0; matrix products, arithmetic and copies ran while one was open for 1% -> 0% of each run, Pallas kernels for 0% -> 0%
where the time goes in v1:
time: 77.2 us; the launch traced here: 77.1 us
  Pallas kernels  73.1 us (95%)
  local copies, waits for them, and re-layouts  3.32 us (4%)
    pallas_call x1, Pallas kernels, local(): pl.pallas_call(functools.partial(kernel, cfg), out_shape=(out, out), in_s...  73.1 us
    unnamed x4, local copies, waits for them, and re-layouts  3.32 us

profile of v1, /device:TPU:0, one launch (start us, length us, event | category | flops | bytes accessed | tf_op | source)
XLA Modules:
  0.0 77.1 jit_solution(18316864618705903898)
XLA Ops:
  0.6 73.1 %shard_map.77 = (bf16[64,8192]{1,0:T(8,128)(2,1)}, bf16[64,8192]{1,0:T(8,128)(2,1)}) custom-call(bf16[256,1024]{1,0:T(8,128)(2,1)} %q_ref.1, bf16[64,512]{1,0:T(8,128)(2,1)} %k_ref.1, bf16[64,512]{1,0:T(8,128)(2,1)} %v_ref.1, bf16[1024,1024]{1,0:T(8,128)(2,1)} %w_ref.1, bf16[64,8192]{1,0:T(8,128)(2,1)} %r_ref.1, f32[1,8192]{1,0:T(1,128)} %bitcast.1), custom_call_target="tpu_custom_call" | custom-call | tf_op jit(solution)/shard_map/pallas_call | solution.py:321
  73.7 0.0 copy-start
  73.8 2.4 %copy.10 = bf16[64,8192]{1,0:T(8,128)(2,1)} copy(bf16[64,8192]{1,0:T(8,128)(2,1)} %get-tuple-element.4) | data formatting | bytes 2097152
  76.1 0.0 copy-done
  76.1 1.0 %copy.11 = bf16[64,8192]{1,0:T(8,128)(2,1)} copy(bf16[64,8192]{1,0:T(8,128)(2,1)S(1)} %copy-done) | data formatting | bytes 2097152
Async XLA Ops:
  73.7 2.4 %copy-start = (bf16[64,8192]{1,0:T(8,128)(2,1)S(1)}, bf16[64,8192]{1,0:T(8,128)(2,1)}, u32[]{:S(2)}) copy-start(bf16[64,8192]{1,0:T(8,128)(2,1)} %get-tuple-element.5) | copy-start | bytes 3145732

commit v2 on v1

--- a/solution.py
+++ b/solution.py
@@ -62,15 +62,14 @@
     return [(k, c) for _, k, c in units], [event for _, _, event in events]
 
 
-def kernel(cfg, q_ref, k_ref, v_ref, w_ref, r_ref, g_ref, hid_ref, nrm_ref,
-           q_v, k_v, v_v, att, w_v, r_v, g_v, keeps, sends, recvs, fin, fin_snd, upd, hid_v, nrm_v,
-           loc_sem, kv_snd, kv_rcv, g_snd, g_rcv, w_snd, w_rcv, s_snd, s_rcv, f_snd, f_rcv, o_sem):
+def kernel(cfg, q_ref, k_ref, v_ref, w_ref, out_ref,
+           q_v, k_v, v_v, att, w_v, keeps, sends, recvs, fin_snd,
+           loc_sem, kv_snd, kv_rcv, g_snd, g_rcv, w_snd, w_rcv, s_snd, s_rcv, f_snd, f_rcv):
     tp, dp, line, blocks, pieces, halves, stages = cfg
     rows, width = q_v.shape
     cols = w_v.shape[2]
     own_cols = cols * pieces
     tok = rows // tp
-    features = fin.shape[1]
     me_dp, me = lax.axis_index("dp"), lax.axis_index("tp")
     a, b = me_dp // blocks, me_dp % blocks
     slot = [reverse(i, stages) for i in range(tp)]
@@ -100,7 +99,6 @@
     first.append(local(k_ref.at[:, aligned(head * HDIM, HDIM)], k_v.at[pl.ds(0, tok)]))
     first.append(local(v_ref.at[:, aligned(head * HDIM, HDIM)], v_v.at[pl.ds(0, tok)]))
     w_local = [local(w_ref.at[:, pl.ds(s * cols, cols)], w_v.at[s]) for s in range(pieces)]
-    r_local = [local(r_ref, r_v), local(g_ref, g_v)]
 
     barrier = pltpu.get_barrier_semaphore()
     order = [pick(a, [visit_order(at, line)[k] for at in range(line)]) for k in range(line)]
@@ -199,11 +197,12 @@
         j, s = divmod(c, pieces)
         start = (a * blocks + (b + j) % blocks) * own_cols + s * cols
         lanes = aligned(start, cols)
+        fin_snd[number] = total.astype(BF)
         if k == 0:
-            fin[:, lanes] = total.astype(BF)
-            return
-        fin_snd[number] = total.astype(BF)
-        remote(fin_snd.at[number], fin.at[:, lanes], f_snd.at[number], f_rcv.at[a, c], dev(order[k], b, me)).start()
+            pltpu.make_async_copy(fin_snd.at[number], out_ref.at[:, lanes], f_snd.at[number]).start()
+        else:
+            remote(fin_snd.at[number], out_ref.at[:, lanes], f_snd.at[number], f_rcv.at[a, c],
+                   dev(order[k], b, me)).start()
 
     def exchange(number, stage):
         return remote(sends[stage].at[number], recvs[stage].at[number], s_snd.at[stage, number],
@@ -247,31 +246,10 @@
             total = keeps[extra - 1][number] + recvs[extra - 1][number].astype(F32)
             pass_on(number, extra, total)
 
-    for copy in r_local:
-        copy.wait()
-    squares = jnp.zeros((tok, 1), F32)
-
-    for k in range(line):
-        source = order[k]
+    for k in range(1, line):
         for c in range(blocks * pieces):
-            j, s = divmod(c, pieces)
-            lanes = aligned((source * blocks + (b + j) % blocks) * own_cols + s * cols, cols)
-            if k:
-                remote(fin.at[:, lanes], fin.at[:, lanes], f_snd.at[0], f_rcv.at[source, c],
-                       dev(source, b, me)).wait_recv()
-            now = r_v[:, lanes].astype(F32) + fin[:, lanes].astype(F32)
-            upd[:, lanes] = now
-            hid_v[:, lanes] = now.astype(BF)
-            squares = squares + jnp.sum(now * now, axis=-1, keepdims=True)
-    out_h = pltpu.make_async_copy(hid_v, hid_ref, o_sem.at[0])
-    out_h.start()
-    scale = lax.rsqrt(squares / features + 1e-05)
-    step = min(features, 1024)
-    for n in range(features // step):
-        lanes = pl.ds(n * step, step)
-        nrm_v[:, lanes] = (upd[:, lanes] * scale * g_v[:, lanes]).astype(BF)
-    out_n = pltpu.make_async_copy(nrm_v, nrm_ref, o_sem.at[1])
-    out_n.start()
+            remote(fin_snd.at[0], out_ref.at[:, pl.ds(0, cols)], f_snd.at[0], f_rcv.at[order[k], c],
+                   dev(order[k], b, me)).wait_recv()
 
     for copy in kv:
         copy.wait_send()
@@ -294,10 +272,17 @@
         for stage in range(stages):
             exchange(number, stage).wait_send()
         if k:
-            remote(fin_snd.at[number], fin.at[:, pl.ds(0, cols)], f_snd.at[number], f_rcv.at[a, c],
+            remote(fin_snd.at[number], out_ref.at[:, pl.ds(0, cols)], f_snd.at[number], f_rcv.at[a, c],
                    dev(order[k], b, me)).wait_send()
-    out_h.wait()
-    out_n.wait()
+        else:
+            pltpu.make_async_copy(fin_snd.at[number], out_ref.at[:, pl.ds(0, cols)], f_snd.at[number]).wait()
+
+
+def norm_kernel(p_ref, r_ref, g_ref, hid_ref, nrm_ref):
+    updated = r_ref[...].astype(F32) + p_ref[...].astype(F32)
+    hid_ref[...] = updated.astype(BF)
+    scale = lax.rsqrt(jnp.mean(updated * updated, axis=-1, keepdims=True) + 1e-05)
+    nrm_ref[...] = (updated * scale * g_ref[...]).astype(BF)
 
 
 def local(tp, dp, queries, keys, values, out_weight, residual, norm_gain):
@@ -306,7 +291,7 @@
     tok, features = residual.shape
     blocks = 2 if dp % 2 == 0 else 1
     line = dp // blocks
-    pieces = max(1, min(2, own_cols // 256))
+    pieces = max(1, min(4, own_cols // 256))
     cols = own_cols // pieces
     halves = 2 if tok % LEN == 0 else 1
     stages = tp.bit_length() - 1
@@ -318,27 +303,34 @@
     cfg = (tp, dp, line, blocks, pieces, halves, stages)
     parts = [rows >> (stage + 1) for stage in range(stages)]
     out = jax.ShapeDtypeStruct((tok, features), BF)
-    return pl.pallas_call(
+    projected = pl.pallas_call(
         functools.partial(kernel, cfg),
-        out_shape=(out, out),
-        in_specs=[any_] * 6,
-        out_specs=(any_, any_),
+        out_shape=out,
+        in_specs=[any_] * 4,
+        out_specs=any_,
         scratch_shapes=[
             vm((rows, width), BF), vm((rows, HDIM), BF), vm((rows, HDIM), BF),
             vm((line, rows, width), BF), vm((chunks, width, cols), BF),
-            vm((tok, features), BF), vm((1, features), F32),
             tuple(vm((count, part, cols), F32) for part in parts),
             tuple(vm((count, part, cols), BF) for part in parts),
             tuple(vm((count, part, cols), BF) for part in parts),
-            vm((tok, features), BF), vm((count, tok, cols), BF), vm((tok, features), F32),
-            vm((tok, features), BF), vm((tok, features), BF),
-            dma((tp + 4 + pieces,)), dma((2, tp)), dma((2, tp)),
+            vm((count, tok, cols), BF),
+            dma((tp + 2 + pieces,)), dma((2, tp)), dma((2, tp)),
             dma((line, halves, 2)), dma((line, halves)), dma((chunks,)), dma((chunks,)),
-            dma((stages, count)), dma((stages, count)), dma((count,)), dma((line, chunks)), dma((2,)),
+            dma((stages, count)), dma((stages, count)), dma((count,)), dma((line, chunks)),
         ],
         compiler_params=pltpu.CompilerParams(
             collective_id=0, has_side_effects=True, vmem_limit_bytes=56 * 1024 * 1024),
-    )(queries, keys, values, out_weight, residual, norm_gain.reshape(1, features))
+    )(queries, keys, values, out_weight)
+    high = min(16, tok)
+    block = pl.BlockSpec((high, features), lambda i: (i, 0))
+    return pl.pallas_call(
+        norm_kernel,
+        grid=(tok // high,),
+        out_shape=(out, out),
+        in_specs=[block, block, pl.BlockSpec((1, features), lambda i: (0, 0))],
+        out_specs=(block, block),
+    )(projected, residual, norm_gain.reshape(1, features))
 
 
 def solution(mesh):

time: 77.2 us -> 74.3 us (0.962)
  local copies, waits for them, and re-layouts: 3.32 us -> 0 us
    unnamed x4 -> x0, local copies, waits for them, and re-layouts: 3.32 us -> none
    pallas_call x1 -> x2, Pallas kernels: 73.1 us -> 73.5 us  [the longest x1 69.5 us: local(): pl.pallas_call(functools.partial(kernel, cfg), out_shape=out, in_specs=[a...]
where the time goes in v2:
time: 74.3 us; the launch traced here: 74.1 us
  Pallas kernels  73.5 us (99%)
    pallas_call x1, Pallas kernels, local(): pl.pallas_call(functools.partial(kernel, cfg), out_shape=out, in_specs=[a...  69.5 us
    pallas_call x1, Pallas kernels, local(): pl.pallas_call(norm_kernel, grid=(tok // high,), out_shape=(out, out), in...  4 us

profile of v2, /device:TPU:0, one launch (start us, length us, event | category | flops | bytes accessed | tf_op | source)
XLA Modules:
  0.0 74.1 jit_solution(16305076717748198484)
XLA Ops:
  0.6 69.5 %shard_map.77.p_ref = bf16[64,8192]{1,0:T(8,128)(2,1)} custom-call(bf16[256,1024]{1,0:T(8,128)(2,1)} %q_ref.1, bf16[64,512]{1,0:T(8,128)(2,1)} %k_ref.1, bf16[64,512]{1,0:T(8,128)(2,1)} %v_ref.1, bf16[1024,1024]{1,0:T(8,128)(2,1)} %w_ref.1), custom_call_target="tpu_custom_call" | custom-call | tf_op jit(solution)/shard_map/pallas_call | solution.py:306
  70.1 4.0 %shard_map.78 = (bf16[64,8192]{1,0:T(8,128)(2,1)}, bf16[64,8192]{1,0:T(8,128)(2,1)}) custom-call(bf16[64,8192]{1,0:T(8,128)(2,1)} %shard_map.77.p_ref, bf16[64,8192]{1,0:T(8,128)(2,1)} %r_ref.1, f32[1,8192]{1,0:T(1,128)} %bitcast.1), custom_call_target="tpu_custom_call" | custom-call | tf_op jit(solution)/shard_map/pallas_call | solution.py:327
